TPU v7x, 32 devices: a whole 2x2x4 slice. The times are simulated.
32 devices in a mesh: pts: 8 (over z, y), cam: 4 (over x, core).
Axes of the slice: x: 2, y: 2, z: 4, core: 2. Of those that a mesh axis runs over, the one named last changes fastest.
Arguments:
- feat_res: bfloat16 [16, 128, 16384], P(None, None, ('pts', 'cam')), may hold values from -6 to 6
- feat_grad: bfloat16 [2, 16, 128, 16384], P(None, None, None, ('pts', 'cam')), may hold values from -0.125 to 0.125
- cam_jac: float32 [2, 6, 16384], P(None, None, ('pts', 'cam')), may hold values from -6 to 6
- pt_jac: float32 [2, 3, 16384], P(None, None, ('pts', 'cam')), may hold values from -6 to 6
- obs_camera: int32 [16384], P(('pts', 'cam')), may hold values from 0 to 255
- point_counts: int32 [32, 128], P(('pts', 'cam')), may hold values from 1 to 16, 512 in all within a row
Outputs:
- camera_step: float32 [6, 256], replicated
- point_step: float32 [3, 4096], P(None, ('pts', 'cam'))
Inputs may be any that keep to these rules, and one draw needn't show every extreme that they name: Each row of point_counts sums to 512, so every point's observations lie on the device that holds the point.
All inputs are finite; a program needn't handle non-finite values.
Results may differ from a plain program's by a relative error of at most 0.0003.
Values sent between devices are 32-bit elements; how exact they have to be, the bound alone decides.
A program may use at most 128 MiB of HBM per device.

v0:
```python
import jax
import jax.numpy as jnp
from jax import lax
from jax.sharding import PartitionSpec as P

CAM_DEV = 8
ITERS = 4


damping = 1.0
highest = lax.Precision.HIGHEST


def feature_terms(residual, gradient):
    energy = jnp.einsum("pcn,pcn->n", residual, residual, preferred_element_type=jnp.float32)
    moment = jnp.einsum("apcn,bpcn->abn", gradient, gradient, preferred_element_type=jnp.float32)
    pulled = jnp.einsum("apcn,pcn->an", gradient, residual, preferred_element_type=jnp.float32)
    weight = 1.0 / (1.0 + energy / (residual.shape[0] * residual.shape[1]))
    return (moment * weight, pulled * weight)


def segment_total(values, indices, segments):
    return jax.ops.segment_sum(values.T, indices, num_segments=segments).T


def cholesky_rows(matrix, dimension):
    factor = [[None] * dimension for position in range(dimension)]
    for column in range(dimension):
        pivot_value = matrix[column][column]
        for earlier in range(column):
            pivot_value = pivot_value - factor[column][earlier] * factor[column][earlier]
        factor[column][column] = jnp.sqrt(pivot_value)
        for lower_row in range(column + 1, dimension):
            element = matrix[lower_row][column]
            for earlier in range(column):
                element = element - factor[lower_row][earlier] * factor[column][earlier]
            factor[lower_row][column] = element / factor[column][column]
    return factor


def take_factor(factor, indices):
    picked = []
    for row_list in factor:
        picked.append([None if element is None else element[indices] for element in row_list])
    return picked


def cholesky_solve(factor, right_side):
    dimension = len(factor)
    forward = []
    for column in range(dimension):
        element = right_side[column]
        for earlier in range(column):
            element = element - factor[column][earlier] * forward[earlier]
        forward.append(element / factor[column][column])
    backward = [None] * dimension
    for column in reversed(range(dimension)):
        element = forward[column]
        for latter in range(column + 1, dimension):
            element = element - factor[latter][column] * backward[latter]
        backward[column] = element / factor[column][column]
    return jnp.stack(backward)


def point_system(moment, pulled, pt_jac, point_ids, segments):
    weighted = jnp.einsum("abn,bjn->ajn", moment, pt_jac, precision=highest)
    blocks = jnp.einsum("ain,ajn->ijn", pt_jac, weighted, precision=highest)
    point_force = jnp.einsum("ain,an->in", pt_jac, pulled, precision=highest)
    summed = segment_total(
        jnp.concatenate([blocks.reshape(9, -1), point_force]), point_ids, segments
    )
    hessian = summed[:9].reshape(3, 3, -1) + damping * jnp.eye(3, dtype=jnp.float32)[:, :, None]
    return (cholesky_rows(hessian, 3), summed[9:])


def camera_terms(moment, pulled, cam_jac, pt_jac, point_factor, point_force, point_ids):
    local_factor = take_factor(point_factor, point_ids)
    toward = jnp.einsum("abn,bjn->ajn", moment, cam_jac, precision=highest)
    camera_block = jnp.einsum("ain,ajn->ijn", cam_jac, toward, precision=highest)
    coupling = jnp.einsum("ain,ajn->ijn", pt_jac, toward, precision=highest)
    solved = cholesky_solve(local_factor, coupling)
    reduced = camera_block - jnp.einsum("kin,kjn->ijn", coupling, solved, precision=highest)
    point_shift = cholesky_solve(point_factor, point_force)[:, point_ids]
    pointward = jnp.einsum("abn,bjn->ajn", moment, pt_jac, precision=highest)
    leftover = pulled - jnp.einsum("ajn,jn->an", pointward, point_shift, precision=highest)
    gradient = jnp.einsum("ain,an->in", cam_jac, leftover, precision=highest)
    return jnp.concatenate([reduced.reshape(36, -1), gradient])


def camera_image(
    values, moment, cam_jac, pt_jac, point_factor, point_ids, slot_ids, point_total, slot_total
):
    at_obs = values[:, slot_ids]
    projected = jnp.einsum("ajn,jn->an", cam_jac, at_obs, precision=highest)
    pushed = jnp.einsum("abn,bn->an", moment, projected, precision=highest)
    gathered = segment_total(
        jnp.einsum("ain,an->in", pt_jac, pushed, precision=highest), point_ids, point_total
    )
    answer = cholesky_solve(point_factor, gathered)[:, point_ids]
    remain = projected - jnp.einsum("ajn,jn->an", pt_jac, answer, precision=highest)
    image_terms = jnp.einsum("ain,abn,bn->in", cam_jac, moment, remain, precision=highest)
    return segment_total(image_terms, slot_ids, slot_total)


def point_update(
    values, moment, pulled, cam_jac, pt_jac, point_factor, point_ids, slot_ids, point_total
):
    projected = jnp.einsum("ajn,jn->an", cam_jac, values[:, slot_ids], precision=highest)
    pushed = pulled + jnp.einsum("abn,bn->an", moment, projected, precision=highest)
    point_force = segment_total(
        jnp.einsum("ain,an->in", pt_jac, pushed, precision=highest), point_ids, point_total
    )
    return -cholesky_solve(point_factor, point_force)


def camera_factor_of(camera_sums):
    matrix = (
        camera_sums[:36].reshape(6, 6, -1) + damping * jnp.eye(6, dtype=jnp.float32)[:, :, None]
    )
    return cholesky_rows(matrix, 6)


def shards(feat_res, feat_grad, cam_jac, pt_jac, obs_camera, point_counts):
    moment, pulled = feature_terms(feat_res, feat_grad)
    observations = pulled.shape[1]
    point_total = point_counts.shape[1]
    slot_total = CAM_DEV * lax.axis_size(("pts", "cam"))
    ends = jnp.cumsum(point_counts[0])
    point_ids = jnp.searchsorted(ends, jnp.arange(observations, dtype=jnp.int32), side="right")
    point_factor, point_force = point_system(moment, pulled, pt_jac, point_ids, point_total)
    local_sums = segment_total(
        camera_terms(moment, pulled, cam_jac, pt_jac, point_factor, point_force, point_ids),
        obs_camera,
        slot_total,
    )
    camera_sums = lax.psum(local_sums, ("pts", "cam"))
    camera_factor = camera_factor_of(camera_sums)

    def apply_system(direction):
        local_image = camera_image(
            direction,
            moment,
            cam_jac,
            pt_jac,
            point_factor,
            point_ids,
            obs_camera,
            point_total,
            slot_total,
        )
        image = lax.psum(local_image, ("pts", "cam"))
        return image + damping * direction

    def curvature_of(direction, image):
        local_value = jnp.sum(direction * image)
        return local_value

    def progress_of(remaining, precond):
        local_value = jnp.sum(remaining * precond)
        return local_value

    remaining = -camera_sums[36:]
    precond = cholesky_solve(camera_factor, remaining)
    progress = progress_of(remaining, precond)

    def iterate(step_index, state_tuple):
        solution, remaining, direction, progress = state_tuple
        image = apply_system(direction)
        alpha_value = progress / curvature_of(direction, image)
        solution = solution + alpha_value * direction
        remaining = remaining - alpha_value * image
        precond = cholesky_solve(camera_factor, remaining)
        renewed = progress_of(remaining, precond)
        direction = precond + renewed / progress * direction
        return (solution, remaining, direction, renewed)

    solution, remaining, direction, progress = lax.fori_loop(
        0, ITERS, iterate, (jnp.zeros_like(remaining), remaining, precond, progress)
    )
    point_step = point_update(
        solution, moment, pulled, cam_jac, pt_jac, point_factor, point_ids, obs_camera, point_total
    )
    return (solution, point_step)


def solution(mesh):
    return jax.shard_map(
        shards,
        mesh=mesh,
        in_specs=(
            P(None, None, ("pts", "cam")),
            P(None, None, None, ("pts", "cam")),
            P(None, None, ("pts", "cam")),
            P(None, None, ("pts", "cam")),
            P(("pts", "cam")),
            P(("pts", "cam"), None),
        ),
        out_specs=(P(), P(None, ("pts", "cam"))),
        check_vma=False,
    )
```

profile of v0, /device:TPU:0, one launch (start us, length us, event | category | flops | bytes accessed | tf_op | source)
XLA Modules:
  0.0 567.1 jit_solution(15435472559805765553)
XLA Ops:
  1.7 27.5 %while.44 = (s32[]{:T(128)}, u32[512]{0:T(512)S(1)}, u32[512]{0:T(512)S(1)}, s32[128]{0:T(128)S(1)}, s32[]{:T(128)}, /*index=5*/s32[]{:T(128)}, s32[]{}) while((s32[]{:T(128)}, u32[512]{0:T(512)S(1)}, u32[512]{0:T(512)S(1)}, s32[128]{0:T(128)S(1)}, s32[]{:T(128)}, /*index=5*/s32[]{:T(128)}, s32[]{}) %tuple.189), condition=%wide.region_2.3_spmd.clone, body=%wide.region_1.2_spmd.clone.sunk | while | flops 10244 | bytes 37997 | solution.py:129
  29.3 7.6 %copy.739 = bf16[16,128,512,1]{1,3,0,2:T(2,128)(2,1)} copy(bf16[16,128,512,1]{2,1,0,3:T(8,128)(2,1)S(1)} %bitcast.675) | data formatting | bytes 4194304 | tf_op args[0]
  36.9 11.3 %copy.693 = bf16[2,16,128,512]{2,0,1,3:T(2,128)(2,1)} copy(bf16[2,16,128,512]{3,2,1,0:T(8,128)(2,1)} %param.11) | data formatting | bytes 8388608 | tf_op args[1]
  48.3 14.0 %fusion.108 = f32[512,1,2,1]{2,1,3,0:T(1,128)S(1)} fusion(bf16[16,128,512,1]{1,3,0,2:T(2,128)(2,1)} %copy.739, bf16[2,16,128,512]{2,0,1,3:T(2,128)(2,1)} %copy.693), kind=kOutput, calls=%fused_computation.277 | convolution fusion | flops 4194304 | bytes 6295552 | tf_op jit(solution)/shard_map/apcn,pcn->an/dot_general | solution.py:17
  63.2 3.6 fusion.109
  67.0 14.9 %fusion.28 = f32[2,2,512]{0,1,2:T(2,128)S(1)} fusion(bf16[2,16,128,512]{2,0,1,3:T(2,128)(2,1)} %copy.693, f32[512]{0:T(512)S(1)} %add_divide_fusion), kind=kOutput, calls=%fused_computation.88 | convolution fusion | flops 8390656 | bytes 4204544 | tf_op jit(solution)/shard_map/apcn,bpcn->abn/dot_general | solution.py:16
  81.9 4.5 convolution_bitcast_fusion.4
  86.4 4.2 convolution_bitcast_fusion.2
  91.2 3.5 scatter_custom_fusion.2
  97.2 3.5 fusion.110
  104.8 4.5 convolution_bitcast_fusion.5
  109.3 4.5 fusion.106
  113.7 5.3 fusion.107
  120.9 4.5 gather_fusion.5
  125.4 4.5 gather_fusion.4
  130.6 4.5 gather_fusion.3
  136.4 4.4 gather_fusion.7
  140.8 4.5 gather_fusion.6
  145.3 4.8 gather_fusion.8
  153.1 6.9 %subtract_bitcast_fusion = f32[6,6,512]{0,1,2:T(8,128)} fusion(f32[512,6,6]{2,1,0:T(8,128)S(1)} %fusion.106, f32[3,6,512]{1,0,2:T(4,128)} %copy.707, f32[512,6,3]{1,2,0:T(4,128)S(1)} %fusion.107), kind=kOutput, calls=%fused_computation.81 | convolution fusion | flops 681984 | bytes 221184 | tf_op jit(solution)/shard_map/kin,kjn->ijn/dot_general | solution.py:82
  164.8 42.4 %psum.17 = f32[42,256]{1,0:T(8,128)S(1)} all-reduce(f32[42,256]{1,0:T(8,128)S(1)} %bitcast.690), channel_id=1, replica_groups=mesh['pts'=8,'cam'=4] {'pts','cam'}, use_global_device_ids=true, to_apply=%region_5.6 | all-reduce | flops 10752 | bytes 86016 | tf_op jit(solution)/shard_map/psum | solution.py:136
  208.6 340.7 %while.45 = (s32[]{:T(128)}, f32[6,256]{1,0:T(8,128)S(1)}, f32[6,256]{1,0:T(8,128)S(1)}, f32[6,256]{1,0:T(8,128)S(1)}, f32[]{:T(128)}, /*index=5*/s32[512]{0:T(5...) while((s32[]{:T(128)}, f32[6,256]{1,0:T(8,128)S(1)}, ...), condition=%wide.region_13.14_spmd.clone, body=%wide.region_7.13_spmd.clone.sunk | while | flops 322179 | bytes 539551 | solution.py:177
  228.7 3.6 fusion.185
  232.5 4.2 convolution_bitcast_fusion.9
  237.0 5.2 fusion.186
  242.2 3.9 scatter_custom_fusion.18
  248.0 4.5 fusion.188
  262.0 40.1 %psum.20 = f32[6,256]{1,0:T(8,128)S(1)} all-reduce(f32[6,256]{1,0:T(8,128)S(1)} %bitcast.682), channel_id=1, replica_groups=mesh['pts'=8,'cam'=4] {'pts','cam'}, use_global_device_ids=true, to_apply=%region_10.10 | all-reduce | flops 1536 | bytes 12288 | tf_op jit(solution)/shard_map/while/body/eval_jaxpr/psum | solution.py:151
  307.0 3.6 fusion.185
  310.8 4.2 convolution_bitcast_fusion.9
  315.3 5.2 fusion.186
  320.5 3.9 scatter_custom_fusion.18
  326.3 4.5 fusion.188
  340.3 39.9 %psum.20 = f32[6,256]{1,0:T(8,128)S(1)} all-reduce(f32[6,256]{1,0:T(8,128)S(1)} %bitcast.682), channel_id=1, replica_groups=mesh['pts'=8,'cam'=4] {'pts','cam'}, use_global_device_ids=true, to_apply=%region_10.10 | all-reduce | flops 1536 | bytes 12288 | tf_op jit(solution)/shard_map/while/body/eval_jaxpr/psum | solution.py:151
  385.1 3.6 fusion.185
  388.9 4.2 convolution_bitcast_fusion.9
  393.4 5.2 fusion.186
  398.6 3.9 scatter_custom_fusion.18
  404.4 4.5 fusion.188
  418.4 40.1 %psum.20 = f32[6,256]{1,0:T(8,128)S(1)} all-reduce(f32[6,256]{1,0:T(8,128)S(1)} %bitcast.682), channel_id=1, replica_groups=mesh['pts'=8,'cam'=4] {'pts','cam'}, use_global_device_ids=true, to_apply=%region_10.10 | all-reduce | flops 1536 | bytes 12288 | tf_op jit(solution)/shard_map/while/body/eval_jaxpr/psum | solution.py:151
  463.3 3.6 fusion.185
  467.1 4.2 convolution_bitcast_fusion.9
  471.6 5.2 fusion.186
  476.8 3.9 scatter_custom_fusion.18
  482.6 4.5 fusion.188
  496.6 39.9 %psum.20 = f32[6,256]{1,0:T(8,128)S(1)} all-reduce(f32[6,256]{1,0:T(8,128)S(1)} %bitcast.682), channel_id=1, replica_groups=mesh['pts'=8,'cam'=4] {'pts','cam'}, use_global_device_ids=true, to_apply=%region_10.10 | all-reduce | flops 1536 | bytes 12288 | tf_op jit(solution)/shard_map/while/body/eval_jaxpr/psum | solution.py:151
  550.6 3.6 convolution_bitcast_fusion.6
  561.3 3.5 scatter_custom_fusion.4
  (261 shorter events, 117.9 us)
Async XLA Ops:
  1.7 27.6 %copy-start = (bf16[16,128,512]{2,1,0:T(8,128)(2,1)S(1)}, bf16[16,128,512]{2,1,0:T(8,128)(2,1)}, u32[]{:S(2)}) copy-start(bf16[16,128,512]{2,1,0:T(8,128)(2,1)} %param.10) | copy-start | bytes 6291460
  48.3 14.7 %copy-start.8 = (f32[2,3,512]{2,0,1:T(2,128)S(1)}, f32[2,3,512]{2,0,1:T(2,128)}, u32[]{:S(2)}) copy-start(f32[2,3,512]{2,0,1:T(2,128)} %param.13) | copy-start | bytes 36868
  63.2 23.2 %copy-start.1 = (f32[2,3,512]{1,0,2:T(2,128)}, f32[2,3,512]{1,0,2:T(2,128)S(1)}, u32[]{:S(2)}) copy-start(f32[2,3,512]{1,0,2:T(2,128)S(1)} %copy.698) | copy-start | bytes 36868
  81.9 22.9 %copy-start.6 = (f32[2,2,512]{0,1,2:T(2,128)}, f32[2,2,512]{0,1,2:T(2,128)S(1)}, u32[]{:S(2)}) copy-start(f32[2,2,512]{0,1,2:T(2,128)S(1)} %fusion.28) | copy-start | bytes 24580
  81.9 18.9 %copy-start.5 = (f32[2,6,512]{2,0,1:T(2,128)S(1)}, f32[2,6,512]{2,0,1:T(2,128)}, u32[]{:S(2)}) copy-start(f32[2,6,512]{2,0,1:T(2,128)} %param.12) | copy-start | bytes 73732
  94.9 18.8 %copy-start.11 = (f32[3,3,128]{2,1,0:T(4,128)}, f32[3,3,128]{2,1,0:T(4,128)S(1)}, u32[]{:S(2)}) copy-start(f32[3,3,128]{2,1,0:T(4,128)S(1)} %broadcast_add_fusion.1) | copy-start | bytes 13828
  95.0 0.6 copy-start.13
  101.1 8.1 %copy-start.3 = (f32[2,6,512]{1,0,2:T(2,128)}, f32[2,6,512]{1,0,2:T(2,128)S(1)}, u32[]{:S(2)}) copy-start(f32[2,6,512]{1,0,2:T(2,128)S(1)} %copy.696) | copy-start | bytes 73732
  153.1 9.3 %copy-start.10 = (s32[512]{0:T(512)S(1)}, s32[512]{0:T(512)}, u32[]{:S(2)}) copy-start(s32[512]{0:T(512)} %param.14) | copy-start | bytes 6148
  153.1 55.5 %copy-start.12 = (f32[1,128]{1,0:T(1,128)S(1)}, f32[1,128]{1,0:T(1,128)}, u32[]{:S(2)}) copy-start(f32[1,128]{1,0:T(1,128)} %get-tuple-element.1652) | copy-start | bytes 1540
  160.0 48.2 %copy-start.7 = (f32[2,2,512]{0,1,2:T(2,128)S(1)}, f32[2,2,512]{0,1,2:T(2,128)}, u32[]{:S(2)}) copy-start(f32[2,2,512]{0,1,2:T(2,128)} %copy-done.6) | copy-start | bytes 24580
  208.6 342.0 %copy-start.4 = (f32[2,6,512]{1,0,2:T(2,128)S(1)}, f32[2,6,512]{1,0,2:T(2,128)}, u32[]{:S(2)}) copy-start(f32[2,6,512]{1,0,2:T(2,128)} %copy-done.3) | copy-start | bytes 73732
  549.4 17.6 %copy-start.9 = (f32[6,256]{1,0:T(8,128)}, f32[6,256]{1,0:T(8,128)S(1)}, u32[]{:S(2)}) copy-start(f32[6,256]{1,0:T(8,128)S(1)} %get-tuple-element.1048) | copy-start | bytes 18436
  549.4 8.5 %copy-start.2 = (f32[2,3,512]{1,0,2:T(2,128)S(1)}, f32[2,3,512]{1,0,2:T(2,128)}, u32[]{:S(2)}) copy-start(f32[2,3,512]{1,0,2:T(2,128)} %copy-done.1) | copy-start | bytes 36868
  549.4 15.5 %copy-start.14 = (f32[1,128]{1,0:T(1,128)S(1)}, f32[1,128]{1,0:T(1,128)}, u32[]{:S(2)}) copy-start(f32[1,128]{1,0:T(1,128)} %copy-done.13) | copy-start | bytes 1540
  549.4 16.3 %copy-start.15 = (f32[1,128]{1,0:T(1,128)S(1)}, f32[1,128]{1,0:T(1,128)}, u32[]{:S(2)}) copy-start(f32[1,128]{1,0:T(1,128)} %get-tuple-element.1294) | copy-start | bytes 1540
where the time goes:
time: 578 us; the launch traced here: 567 us
  blocking collectives  202 us (35%)
  matrix products  178 us (31%)
  local copies, waits for them, and re-layouts  98.5 us (17%)
  other arithmetic  49.6 us (9%)
  loops' own time  37.2 us (6%)
    psum x4, blocking collectives, apply_system(): image = lax.psum(local_image, ('pts', 'cam'))  160 us
    psum x1, blocking collectives, shards(): camera_sums = lax.psum(local_sums, ('pts', 'cam'))  42.4 us
    another operation x1, loops' own time, shards(): lax.fori_loop(0, ITERS, iterate, (jnp.zeros_like(remaining), remaining, p...  36.8 us
    scatter-add x11, other arithmetic, segment_total(): return jax.ops.segment_sum(values.T, indices, num_segments=segments).T  34.1 us
    dot_general x8, matrix products, camera_image(): jnp.einsum('ain,abn,bn->in', cam_jac, moment, remain, precision=highest)  28.2 us
    gather x6, local copies, waits for them, and re-layouts, take_factor(): element[indices]  27.2 us
    gather x8, local copies, waits for them, and re-layouts, shards(): jnp.searchsorted(ends, jnp.arange(observations, dtype=jnp.int32), side='r...  26.8 us
    dot_general x4, matrix products, camera_image(): jnp.einsum('ain,an->in', pt_jac, pushed, precision=highest)  20.7 us

commit v1 on v0

v1 whole, which is shorter than its diff:
```python
import jax
import jax.numpy as jnp
from jax import lax
from jax.experimental import pallas as pl
from jax.experimental.pallas import tpu as pltpu
from jax.sharding import PartitionSpec as P

CAM_DEV = 8
ITERS = 4
CHUNK = 4
AXES = ("cam", "pts")
MESH = pl.DeviceIdType.MESH
f32 = jnp.float32
bf16 = jnp.bfloat16


def feature_kernel(res_ref, grad_ref, out_ref, acc_ref):
    step = pl.program_id(0)
    pixels, channels, width = res_ref.shape
    slabs = channels // 16

    @pl.when(step == 0)
    def _():
        acc_ref[...] = jnp.zeros_like(acc_ref)

    def fold(value):
        return value[:8] + value[8:]

    def pixel(index, carry):
        sums = list(carry)
        for slab in range(slabs):
            rows = slice(16 * slab, 16 * slab + 16)
            r = res_ref[index, rows, :].astype(f32)
            gx = grad_ref[0, index, rows, :].astype(f32)
            gy = grad_ref[1, index, rows, :].astype(f32)
            for spot, (one, two) in enumerate(
                ((r, r), (gx, gx), (gx, gy), (gy, gy), (gx, r), (gy, r))
            ):
                sums[spot] = sums[spot] + fold(one * two)
        return tuple(sums)

    sums = lax.fori_loop(0, pixels, pixel, tuple(acc_ref[spot] for spot in range(6)))
    for spot in range(6):
        acc_ref[spot] = sums[spot]

    @pl.when(step == pl.num_programs(0) - 1)
    def _():
        whole = [jnp.sum(acc_ref[spot], axis=0, keepdims=True) for spot in range(6)]
        weight = 1.0 / (1.0 + whole[0] / (pixels * pl.num_programs(0) * channels))
        rows = [value * weight for value in whole[1:]]
        out_ref[...] = jnp.concatenate(rows + [jnp.zeros((3, width), f32)], axis=0)


def features(feat_res, feat_grad):
    pixels, channels, width = feat_res.shape
    return pl.pallas_call(
        feature_kernel,
        grid=(pixels // CHUNK,),
        in_specs=[
            pl.BlockSpec((CHUNK, channels, width), lambda i: (i, 0, 0)),
            pl.BlockSpec((2, CHUNK, channels, width), lambda i: (0, i, 0, 0)),
        ],
        out_specs=pl.BlockSpec((8, width), lambda i: (0, 0)),
        out_shape=jax.ShapeDtypeStruct((8, width), f32),
        scratch_shapes=[pltpu.VMEM((6, 8, width), f32)],
    )(feat_res, feat_grad)


def exact_dot(value, table, contract):
    rows = value.shape[0]
    high = value.astype(bf16).astype(f32)
    rest = value - high
    middle = rest.astype(bf16).astype(f32)
    pieces = jnp.concatenate([high, middle, rest - middle], axis=0).astype(bf16)
    product = lax.dot_general(
        pieces, table, (((1,), (contract,)), ((), ())), preferred_element_type=f32
    )
    return (product[:rows] + product[rows : 2 * rows]) + product[2 * rows :]


def pad_rows(rows, total):
    have = sum(row.shape[0] for row in rows)
    return jnp.concatenate(rows + [jnp.zeros((total - have, rows[0].shape[1]), f32)], axis=0)


def add_rows(value):
    return jnp.sum(value, axis=0, keepdims=True)


def add_all(value):
    return jnp.sum(jnp.sum(value, axis=0, keepdims=True), axis=1, keepdims=True)


def table_of(mask):
    return jnp.where(mask, 1.0, 0.0).astype(bf16)


def solver_kernel(sizes, feat_ref, cam_ref, pt_ref, id_ref, count_ref, step_ref, point_ref, *scratch):
    places = {axis: lax.axis_index(axis) for axis in AXES}
    buffers, semaphores = scratch[: 2 * (ITERS + 1)], scratch[2 * (ITERS + 1) :]
    cameras, points, width = step_ref.shape[1], point_ref.shape[1], id_ref.shape[1]

    barrier = pltpu.get_barrier_semaphore()
    for axis in AXES:
        for away in range(1, sizes[axis]):
            other = lax.rem(places[axis] + away, sizes[axis])
            pl.semaphore_signal(barrier, inc=1, device_id={axis: other}, device_id_type=MESH)

    def all_reduce(value, turn):
        for level, axis in enumerate(AXES):
            me, size = places[axis], sizes[axis]
            held = buffers[2 * turn + level]
            sent, arrived = semaphores[2 * level], semaphores[2 * level + 1]
            held[me] = value
            copies = []
            for away in range(1, size):
                copies.append(
                    pltpu.make_async_remote_copy(
                        src_ref=held.at[me],
                        dst_ref=held.at[me],
                        send_sem=sent.at[turn, away - 1],
                        recv_sem=arrived.at[turn, away - 1],
                        device_id={axis: lax.rem(me + away, size)},
                        device_id_type=MESH,
                    )
                )
                copies[-1].start()
            for copy in copies:
                copy.wait()
            value = held[0]
            for position in range(1, size):
                value = value + held[position]
        return value

    cam_table = table_of(lax.broadcasted_iota(jnp.int32, (cameras, width), 0) == id_ref[...])
    counts = count_ref[...].astype(f32)
    upper = lax.broadcasted_iota(jnp.int32, (points, points), 0)
    lower = lax.broadcasted_iota(jnp.int32, (points, points), 1)
    ends = jnp.sum(jnp.where(lower <= upper, counts, 0.0), axis=1, keepdims=True)
    starts = jnp.sum(jnp.where(lower < upper, counts, 0.0), axis=1, keepdims=True)
    spot = lax.broadcasted_iota(jnp.int32, (points, width), 1).astype(f32)
    member = (spot >= starts) & (spot < ends)
    first_table = table_of(spot == starts)
    start_row = add_rows(jnp.where(member, starts, 0.0))
    end_row = add_rows(jnp.where(member, ends, 0.0))
    line = lax.broadcasted_iota(jnp.int32, (width, width), 0).astype(f32)
    same_table = table_of((line >= start_row) & (line < end_row))

    m00, m01, m11, p0, p1 = (feat_ref[row : row + 1, :] for row in range(5))
    jc = [pad_rows([cam_ref[axis]], 8) for axis in range(2)]
    jp = [[pt_ref[axis, row : row + 1, :] for row in range(3)] for axis in range(2)]

    mjp = [
        [m00 * jp[0][k] + m01 * jp[1][k] for k in range(3)],
        [m01 * jp[0][k] + m11 * jp[1][k] for k in range(3)],
    ]
    pairs = [(0, 0), (1, 0), (2, 0), (1, 1), (2, 1), (2, 2)]
    rows = [jp[0][i] * mjp[0][j] + jp[1][i] * mjp[1][j] for i, j in pairs]
    rows += [jp[0][k] * p0 + jp[1][k] * p1 for k in range(3)]
    summed = exact_dot(pad_rows(rows, 16), same_table, 0)
    h00, h10, h20, h11, h21, h22, g0, g1, g2 = (summed[row : row + 1] for row in range(9))
    i0 = 1.0 / jnp.sqrt(h00 + 1.0)
    l10, l20 = h10 * i0, h20 * i0
    i1 = 1.0 / jnp.sqrt((h11 + 1.0) - l10 * l10)
    l21 = (h21 - l20 * l10) * i1
    i2 = 1.0 / jnp.sqrt((h22 + 1.0) - l20 * l20 - l21 * l21)

    def forward(a, b, c):
        a = a * i0
        b = (b - l10 * a) * i1
        return a, b, (c - l20 * a - l21 * b) * i2

    mjc = [m00 * jc[0] + m01 * jc[1], m01 * jc[0] + m11 * jc[1]]
    couple = forward(*(jp[0][k] * mjc[0] + jp[1][k] * mjc[1] for k in range(3)))
    force = forward(g0, g1, g2)

    terms = []
    for row in range(6):
        cut = slice(row, row + 1)
        term = jc[0][cut] * mjc[0] + jc[1][cut] * mjc[1]
        for k in range(3):
            term = term - couple[k][cut] * couple[k]
        terms.append(term)
    term = jc[0] * p0 + jc[1] * p1
    for k in range(3):
        term = term - couple[k] * force[k]
    terms.append(term)
    local = exact_dot(jnp.concatenate(terms, axis=0), cam_table, 1)
    packed = [local[8 * row + row : 8 * row + 6] for row in range(6)] + [local[48:54]]
    packed = pad_rows(packed, 32)

    pl.semaphore_wait(barrier, sum(sizes[axis] - 1 for axis in AXES))
    total = all_reduce(packed, 0)

    offsets = [0, 6, 11, 15, 18, 20, 21]

    def entry(i, j):
        low, high = min(i, j), max(i, j)
        at = offsets[low] + high - low
        return total[at : at + 1]

    level = lax.broadcasted_iota(jnp.int32, (8, cameras), 0)
    inverse = [
        pad_rows([entry(i, j) for j in range(6)], 8) + jnp.where(level == i, 1.0, 0.0)
        for i in range(6)
    ]
    for k in range(6):
        scale = 1.0 / inverse[k][k : k + 1]
        pivot = jnp.where(level == k, scale, inverse[k] * scale)
        for i in range(6):
            if i != k:
                factor = inverse[i][k : k + 1]
                inverse[i] = jnp.where(level == k, 0.0, inverse[i]) - factor * pivot
        inverse[k] = pivot

    def precondition(value):
        answer = inverse[0] * value[0:1]
        for j in range(1, 6):
            answer = answer + inverse[j] * value[j : j + 1]
        return answer

    remaining = -pad_rows([total[21:27]], 8)
    direction = precondition(remaining)
    progress = add_all(remaining * direction)
    solution = jnp.zeros_like(direction)
    reached = list(force)
    for turn in range(1, ITERS + 1):
        at_obs = exact_dot(direction, cam_table, 0)
        projected = [add_rows(jc[axis] * at_obs) for axis in range(2)]
        drawn = [add_rows(couple[k] * at_obs) for k in range(3)]
        pushed = [m00 * projected[0] + m01 * projected[1], m01 * projected[0] + m11 * projected[1]]
        pooled = exact_dot(pad_rows(drawn, 8), same_table, 0)
        pooled = [pooled[k : k + 1] for k in range(3)]
        if turn < ITERS:
            image = jc[0] * pushed[0] + jc[1] * pushed[1]
            for k in range(3):
                image = image - couple[k] * pooled[k]
            image = all_reduce(exact_dot(image, cam_table, 1), turn) + direction
            alpha = progress / add_all(direction * image)
        else:
            value = projected[0] * pushed[0] + projected[1] * pushed[1]
            for k in range(3):
                value = value - drawn[k] * pooled[k]
            short = value[:, 0:128]
            for column in range(1, width // 128):
                short = short + value[:, 128 * column : 128 * column + 128]
            short = all_reduce(pad_rows([short], 8), turn)
            alpha = progress / (add_all(short) + add_all(direction * direction))
        solution = solution + alpha * direction
        reached = [reached[k] + alpha * pooled[k] for k in range(3)]
        if turn < ITERS:
            remaining = remaining - alpha * image
            conditioned = precondition(remaining)
            renewed = add_all(remaining * conditioned)
            direction = conditioned + (renewed / progress) * direction
            progress = renewed

    step_ref[...] = solution[:6]
    b2 = reached[2] * i2
    b1 = (reached[1] - l21 * b2) * i1
    b0 = (reached[0] - l10 * b1 - l20 * b2) * i0
    point_ref[...] = -exact_dot(pad_rows([b0, b1, b2], 8), first_table, 1)[:3]


def solve(sizes, terms, cam_jac, pt_jac, obs_camera, point_counts, cameras):
    points = point_counts.shape[1]
    buffers = []
    for turn in range(ITERS + 1):
        rows = 32 if turn == 0 else 8
        columns = cameras if turn < ITERS else 128
        buffers += [pltpu.VMEM((sizes[axis], rows, columns), f32) for axis in AXES]
    semaphores = []
    for axis in AXES:
        semaphores += [pltpu.SemaphoreType.DMA((ITERS + 1, max(sizes[axis] - 1, 1)))] * 2

    def kernel(*refs):
        solver_kernel(sizes, *refs)

    return pl.pallas_call(
        kernel,
        in_specs=[pl.BlockSpec(memory_space=pltpu.VMEM)] * 5,
        out_specs=[pl.BlockSpec(memory_space=pltpu.VMEM)] * 2,
        out_shape=[
            jax.ShapeDtypeStruct((6, cameras), f32),
            jax.ShapeDtypeStruct((3, points), f32),
        ],
        scratch_shapes=buffers + semaphores,
        compiler_params=pltpu.CompilerParams(
            collective_id=0, has_side_effects=True, vmem_limit_bytes=48 * 1024 * 1024
        ),
    )(terms, cam_jac, pt_jac, obs_camera.reshape(1, -1), point_counts)


def solution(mesh):
    sizes = {axis: mesh.shape[axis] for axis in AXES}
    cameras = CAM_DEV * sizes["cam"] * sizes["pts"]

    def shards(feat_res, feat_grad, cam_jac, pt_jac, obs_camera, point_counts):
        terms = features(feat_res, feat_grad)
        return tuple(solve(sizes, terms, cam_jac, pt_jac, obs_camera, point_counts, cameras))

    return jax.shard_map(
        shards,
        mesh=mesh,
        in_specs=(
            P(None, None, ("pts", "cam")),
            P(None, None, None, ("pts", "cam")),
            P(None, None, ("pts", "cam")),
            P(None, None, ("pts", "cam")),
            P(("pts", "cam")),
            P(("pts", "cam"), None),
        ),
        out_specs=(P(), P(None, ("pts", "cam"))),
        check_vma=False,
    )
```

time: 578 us -> 55.4 us (0.10); the launches traced: 567 us -> 55.1 us
  blocking collectives: 202 us -> 0 us
  matrix products: 178 us -> 0 us
  local copies, waits for them, and re-layouts: 98.5 us -> 1.92 us
  Pallas kernels: 0 us -> 52.5 us
  other arithmetic: 49.6 us -> 0 us
  loops' own time: 37.2 us -> 0 us
    psum x5 -> x0, blocking collectives: 202 us -> none  [the longest x4 160 us: apply_system(): image = lax.psum(local_image, ('pts', 'cam'))]
    dot_general x38 -> x0, matrix products: 178 us -> none  [the longest x8 28.2 us: camera_image(): jnp.einsum('ain,abn,bn->in', cam_jac, moment, remain, precision=highest)]
    gather x24 -> x0, local copies, waits for them, and re-layouts: 67.1 us -> none  [the longest x6 27.2 us: take_factor(): element[indices]]
    pallas_call x0 -> x2, Pallas kernels: none -> 52.5 us  [the longest x1 47.3 us: solve(): pl.pallas_call(kernel, in_specs=[pl.BlockSpec(memory_space=pltpu.VMEM)] *...]
    another operation x2 -> x0, loops' own time: 37.2 us -> none  [the longest x1 36.8 us: shards(): lax.fori_loop(0, ITERS, iterate, (jnp.zeros_like(remaining), remaining, p...]
    scatter-add x11 -> x0, other arithmetic: 34.1 us -> none  [segment_total(): return jax.ops.segment_sum(values.T, indices, num_segments=segments).T]
    unnamed x37 -> x14, local copies, waits for them, and re-layouts: 19.8 us -> 1.92 us
where the time goes in v1:
time: 55.4 us; the launch traced here: 55.1 us
  Pallas kernels  52.5 us (95%)
  local copies, waits for them, and re-layouts  1.92 us (3%)
  between operations  0.72 us (1%)
    pallas_call x1, Pallas kernels, solve(): pl.pallas_call(kernel, in_specs=[pl.BlockSpec(memory_space=pltpu.VMEM)] *...  47.3 us
    pallas_call x1, Pallas kernels, features(): pl.pallas_call(feature_kernel, grid=(pixels // CHUNK,), in_specs=[pl.Bloc...  5.22 us
    unnamed x14, local copies, waits for them, and re-layouts  1.92 us

profile of v1, /device:TPU:0, one launch (start us, length us, event | category | flops | bytes accessed | tf_op | source)
XLA Modules:
  0.0 55.1 jit_solution(9725952458903355191)
XLA Ops:
  0.6 0.0 copy-start.2
  0.6 0.0 copy-start.1
  0.7 0.0 copy-start.4
  0.7 0.0 copy-start.3
  0.7 5.2 %shard_map.77.refs_0_ = f32[8,512]{1,0:T(8,128)} custom-call(bf16[16,128,512]{2,1,0:T(8,128)(2,1)} %res_ref.1, bf16[2,16,128,512]{3,2,1,0:T(8,128)(2,1)} %grad_ref.1), custom_call_target="tpu_custom_call" | custom-call | tf_op jit(solution)/shard_map/pallas_call | solution.py:56
  5.9 0.0 copy-done.4
  5.9 0.0 copy-done.3
  5.9 0.0 copy-done.2
  5.9 0.0 copy-done.1
  5.9 0.0 copy-start
  6.0 0.7 %copy-done = f32[8,512]{1,0:T(8,128)S(1)} copy-done((f32[8,512]{1,0:T(8,128)S(1)}, f32[8,512]{1,0:T(8,128)}, u32[]{:S(2)}) %copy-start) | copy-done | bytes 16408
  6.7 47.3 %shard_map.78 = (f32[6,256]{1,0:T(8,128)S(1)}, f32[3,128]{1,0:T(4,128)S(1)}) custom-call(f32[8,512]{1,0:T(8,128)S(1)} %copy-done, f32[2,6,512]{2,1,0:T(8,128)S(1)} %copy.8.refs_1_, f32[2,3,512]{2,1,0:T(4,128)S(1)} %copy.9.refs_2_, s32[1,512]{1,0:T(1,128)S(1)} %bitcast.1, s32[1,128]{1,0:T(1,128)S(1)} %copy-done.2), custom_call_target="tpu_custom_call" | custom-call | tf_op jit(solution)/shard_map/pallas_call | solution.py:279
  54.0 0.6 %copy.12 = f32[6,256]{1,0:T(8,128)} copy(f32[6,256]{1,0:T(8,128)S(1)} %get-tuple-element.4) | data formatting | bytes 12288
  54.6 0.6 %copy.13 = f32[3,128]{1,0:T(4,128)} copy(f32[3,128]{1,0:T(4,128)S(1)} %get-tuple-element.5) | data formatting | bytes 3072
  (2 shorter events, 0.0 us)
Async XLA Ops:
  0.6 5.3 %copy-start.2 = (s32[1,128]{1,0:T(1,128)S(1)}, s32[1,128]{1,0:T(1,128)}, u32[]{:S(2)}) copy-start(s32[1,128]{1,0:T(1,128)} %refs_4_.1) | copy-start | bytes 1540
  0.6 5.3 %copy-start.1 = (s32[512]{0:T(512)S(1)}, s32[512]{0:T(512)}, u32[]{:S(2)}) copy-start(s32[512]{0:T(512)} %param.10) | copy-start | bytes 6148
  0.7 5.2 %copy-start.4 = (f32[2,3,512]{2,0,1:T(2,128)S(1)}, f32[2,3,512]{2,0,1:T(2,128)}, u32[]{:S(2)}) copy-start(f32[2,3,512]{2,0,1:T(2,128)} %param.9) | copy-start | bytes 36868
  0.7 5.2 %copy-start.3 = (f32[2,6,512]{2,0,1:T(2,128)S(1)}, f32[2,6,512]{2,0,1:T(2,128)}, u32[]{:S(2)}) copy-start(f32[2,6,512]{2,0,1:T(2,128)} %param.8) | copy-start | bytes 73732
  5.9 0.7 %copy-start = (f32[8,512]{1,0:T(8,128)S(1)}, f32[8,512]{1,0:T(8,128)}, u32[]{:S(2)}) copy-start(f32[8,512]{1,0:T(8,128)} %shard_map.77.refs_0_) | copy-start | bytes 49156

commit v2 on v1

--- a/solution.py
+++ b/solution.py
@@ -7,7 +7,8 @@
 
 CAM_DEV = 8
 ITERS = 4
-CHUNK = 4
+STEPS = 2
+PLANS = (("cam", "pts"),) + (("pair", "chips"),) * 4
 AXES = ("cam", "pts")
 MESH = pl.DeviceIdType.MESH
 f32 = jnp.float32
@@ -55,10 +56,10 @@
     pixels, channels, width = feat_res.shape
     return pl.pallas_call(
         feature_kernel,
-        grid=(pixels // CHUNK,),
+        grid=(STEPS,),
         in_specs=[
-            pl.BlockSpec((CHUNK, channels, width), lambda i: (i, 0, 0)),
-            pl.BlockSpec((2, CHUNK, channels, width), lambda i: (0, i, 0, 0)),
+            pl.BlockSpec((pixels // STEPS, channels, width), lambda i: (i, 0, 0)),
+            pl.BlockSpec((2, pixels // STEPS, channels, width), lambda i: (0, i, 0, 0)),
         ],
         out_specs=pl.BlockSpec((8, width), lambda i: (0, 0)),
         out_shape=jax.ShapeDtypeStruct((8, width), f32),
@@ -95,43 +96,83 @@
     return jnp.where(mask, 1.0, 0.0).astype(bf16)
 
 
-def solver_kernel(sizes, feat_ref, cam_ref, pt_ref, id_ref, count_ref, step_ref, point_ref, *scratch):
+def peer_groups(sizes, pair_axis, places):
+    other_axis = AXES[1 - AXES.index(pair_axis)]
+    half = lax.rem(places[pair_axis], 2)
+    partner = places[pair_axis] + 1 - 2 * half
+    moved = {
+        axis: [places[axis]]
+        + [lax.rem(places[axis] + away, sizes[axis]) for away in range(1, sizes[axis])]
+        for axis in AXES
+    }
+
+    def line(axis):
+        return (
+            {(axis, away): {axis: moved[axis][away]} for away in range(1, sizes[axis])},
+            places[axis],
+        )
+
+    chips = {}
+    for away in reversed(range(sizes[other_axis])):
+        for step in range(0, sizes[pair_axis], 2):
+            if away and step:
+                name = (other_axis, away, step)
+                chips[name] = {other_axis: moved[other_axis][away], pair_axis: moved[pair_axis][step]}
+            elif away:
+                chips[(other_axis, away)] = {other_axis: moved[other_axis][away]}
+            elif step:
+                chips[(pair_axis, step)] = {pair_axis: moved[pair_axis][step]}
+    slot = places[other_axis] * (sizes[pair_axis] // 2) + lax.div(places[pair_axis], 2)
+    return {
+        "cam": line("cam"),
+        "pts": line("pts"),
+        "pair": ({("partner",): {pair_axis: partner}}, half),
+        "chips": (chips, slot),
+    }
+
+
+def solver_kernel(sizes, pair_axis, feat_ref, cam_ref, pt_ref, id_ref, count_ref, step_ref, point_ref, *scratch):
     places = {axis: lax.axis_index(axis) for axis in AXES}
     buffers, semaphores = scratch[: 2 * (ITERS + 1)], scratch[2 * (ITERS + 1) :]
     cameras, points, width = step_ref.shape[1], point_ref.shape[1], id_ref.shape[1]
 
+    groups = peer_groups(sizes, pair_axis, places)
     barrier = pltpu.get_barrier_semaphore()
-    for axis in AXES:
-        for away in range(1, sizes[axis]):
-            other = lax.rem(places[axis] + away, sizes[axis])
-            pl.semaphore_signal(barrier, inc=1, device_id={axis: other}, device_id_type=MESH)
+    greeted = {}
+    for phases in set(PLANS):
+        for offsets, _ in map(groups.get, phases):
+            greeted.update(offsets)
+    for device in greeted.values():
+        pl.semaphore_signal(barrier, inc=1, device_id=device, device_id_type=MESH)
 
     def all_reduce(value, turn):
-        for level, axis in enumerate(AXES):
-            me, size = places[axis], sizes[axis]
+        for level, phase in enumerate(PLANS[turn]):
+            offsets, me = groups[phase]
             held = buffers[2 * turn + level]
-            sent, arrived = semaphores[2 * level], semaphores[2 * level + 1]
+            sent, arrived = semaphores[4 * turn + 2 * level : 4 * turn + 2 * level + 2]
             held[me] = value
             copies = []
-            for away in range(1, size):
+            for spot, device in enumerate(offsets.values()):
                 copies.append(
                     pltpu.make_async_remote_copy(
                         src_ref=held.at[me],
                         dst_ref=held.at[me],
-                        send_sem=sent.at[turn, away - 1],
-                        recv_sem=arrived.at[turn, away - 1],
-                        device_id={axis: lax.rem(me + away, size)},
+                        send_sem=sent.at[spot],
+                        recv_sem=arrived.at[spot],
+                        device_id=device,
                         device_id_type=MESH,
                     )
                 )
                 copies[-1].start()
             for copy in copies:
-                copy.wait()
+                copy.wait_recv()
             value = held[0]
-            for position in range(1, size):
+            for position in range(1, held.shape[0]):
                 value = value + held[position]
+            started.extend(copies)
         return value
 
+    started = []
     cam_table = table_of(lax.broadcasted_iota(jnp.int32, (cameras, width), 0) == id_ref[...])
     counts = count_ref[...].astype(f32)
     upper = lax.broadcasted_iota(jnp.int32, (points, points), 0)
@@ -187,9 +228,9 @@
     terms.append(term)
     local = exact_dot(jnp.concatenate(terms, axis=0), cam_table, 1)
     packed = [local[8 * row + row : 8 * row + 6] for row in range(6)] + [local[48:54]]
-    packed = pad_rows(packed, 32)
-
-    pl.semaphore_wait(barrier, sum(sizes[axis] - 1 for axis in AXES))
+    packed = jnp.concatenate(packed, axis=0)
+
+    pl.semaphore_wait(barrier, len(greeted))
     total = all_reduce(packed, 0)
 
     offsets = [0, 6, 11, 15, 18, 20, 21]
@@ -235,7 +276,8 @@
             image = jc[0] * pushed[0] + jc[1] * pushed[1]
             for k in range(3):
                 image = image - couple[k] * pooled[k]
-            image = all_reduce(exact_dot(image, cam_table, 1), turn) + direction
+            image = all_reduce(exact_dot(image, cam_table, 1)[:6], turn)
+            image = pad_rows([image], 8) + direction
             alpha = progress / add_all(direction * image)
         else:
             value = projected[0] * pushed[0] + projected[1] * pushed[1]
@@ -244,7 +286,7 @@
             short = value[:, 0:128]
             for column in range(1, width // 128):
                 short = short + value[:, 128 * column : 128 * column + 128]
-            short = all_reduce(pad_rows([short], 8), turn)
+            short = all_reduce(short, turn)
             alpha = progress / (add_all(short) + add_all(direction * direction))
         solution = solution + alpha * direction
         reached = [reached[k] + alpha * pooled[k] for k in range(3)]
@@ -256,25 +298,28 @@
             progress = renewed
 
     step_ref[...] = solution[:6]
+    for copy in started:
+        copy.wait_send()
     b2 = reached[2] * i2
     b1 = (reached[1] - l21 * b2) * i1
     b0 = (reached[0] - l10 * b1 - l20 * b2) * i0
     point_ref[...] = -exact_dot(pad_rows([b0, b1, b2], 8), first_table, 1)[:3]
 
 
-def solve(sizes, terms, cam_jac, pt_jac, obs_camera, point_counts, cameras):
+def solve(sizes, pair_axis, terms, cam_jac, pt_jac, obs_camera, point_counts, cameras):
     points = point_counts.shape[1]
-    buffers = []
-    for turn in range(ITERS + 1):
-        rows = 32 if turn == 0 else 8
+    buffers, semaphores = [], []
+    chips = sizes["cam"] * sizes["pts"] // 2
+    members = {"cam": sizes["cam"], "pts": sizes["pts"], "pair": 2, "chips": chips}
+    for turn, phases in enumerate(PLANS):
+        rows = 27 if turn == 0 else 6 if turn < ITERS else 1
         columns = cameras if turn < ITERS else 128
-        buffers += [pltpu.VMEM((sizes[axis], rows, columns), f32) for axis in AXES]
-    semaphores = []
-    for axis in AXES:
-        semaphores += [pltpu.SemaphoreType.DMA((ITERS + 1, max(sizes[axis] - 1, 1)))] * 2
+        for phase in phases:
+            buffers.append(pltpu.VMEM((members[phase], rows, columns), f32))
+            semaphores += [pltpu.SemaphoreType.DMA((members[phase] - 1,))] * 2
 
     def kernel(*refs):
-        solver_kernel(sizes, *refs)
+        solver_kernel(sizes, pair_axis, *refs)
 
     return pl.pallas_call(
         kernel,
@@ -291,13 +336,23 @@
     )(terms, cam_jac, pt_jac, obs_camera.reshape(1, -1), point_counts)
 
 
+def chip_axis(mesh):
+    for axis in AXES:
+        lines = mesh.devices if mesh.axis_names[0] == axis else mesh.devices.T
+        spots = [getattr(device, "coords", None) for device in lines[:2, 0]]
+        if len(spots) == 2 and spots[0] is not None and list(spots[0]) == list(spots[1]):
+            return axis
+    return "cam"
+
+
 def solution(mesh):
     sizes = {axis: mesh.shape[axis] for axis in AXES}
     cameras = CAM_DEV * sizes["cam"] * sizes["pts"]
+    pair_axis = chip_axis(mesh)
 
     def shards(feat_res, feat_grad, cam_jac, pt_jac, obs_camera, point_counts):
         terms = features(feat_res, feat_grad)
-        return tuple(solve(sizes, terms, cam_jac, pt_jac, obs_camera, point_counts, cameras))
+        return tuple(solve(sizes, pair_axis, terms, cam_jac, pt_jac, obs_camera, point_counts, cameras))
 
     return jax.shard_map(
         shards,

time: 55.4 us -> 51.9 us (0.937)
  Pallas kernels: 52.5 us -> 49 us
    pallas_call x1, Pallas kernels: 47.3 us -> 44.3 us  [solve(): pl.pallas_call(kernel, in_specs=[pl.BlockSpec(memory_space=pltpu.VMEM)] *...]
where the time goes in v2:
time: 51.9 us; the launch traced here: 51.7 us
  Pallas kernels  49 us (94%)
  local copies, waits for them, and re-layouts  1.92 us (4%)
  between operations  0.72 us (1%)
    pallas_call x1, Pallas kernels, solve(): pl.pallas_call(kernel, in_specs=[pl.BlockSpec(memory_space=pltpu.VMEM)] *...  44.3 us
    pallas_call x1, Pallas kernels, features(): pl.pallas_call(feature_kernel, grid=(STEPS,), in_specs=[pl.BlockSpec((pix...  4.76 us
    unnamed x14, local copies, waits for them, and re-layouts  1.92 us

profile of v2, /device:TPU:0, one launch (start us, length us, event | category | flops | bytes accessed | tf_op | source)
XLA Modules:
  0.0 51.7 jit_solution(4803743658559025972)
XLA Ops:
  0.6 0.0 copy-start.2
  0.6 0.0 copy-start.1
  0.7 0.0 copy-start.4
  0.7 0.0 copy-start.3
  0.7 4.8 %shard_map.77.refs_0_ = f32[8,512]{1,0:T(8,128)} custom-call(bf16[16,128,512]{2,1,0:T(8,128)(2,1)} %res_ref.1, bf16[2,16,128,512]{3,2,1,0:T(8,128)(2,1)} %grad_ref.1), custom_call_target="tpu_custom_call" | custom-call | tf_op jit(solution)/shard_map/pallas_call | solution.py:57
  5.4 0.0 copy-done.4
  5.4 0.0 copy-done.3
  5.5 0.0 copy-done.2
  5.5 0.0 copy-done.1
  5.5 0.0 copy-start
  5.5 0.7 %copy-done = f32[8,512]{1,0:T(8,128)S(1)} copy-done((f32[8,512]{1,0:T(8,128)S(1)}, f32[8,512]{1,0:T(8,128)}, u32[]{:S(2)}) %copy-start) | copy-done | bytes 16408
  6.2 44.3 %shard_map.78 = (f32[6,256]{1,0:T(8,128)S(1)}, f32[3,128]{1,0:T(4,128)S(1)}) custom-call(f32[8,512]{1,0:T(8,128)S(1)} %copy-done, f32[2,6,512]{2,1,0:T(8,128)S(1)} %copy.8.refs_1_, f32[2,3,512]{2,1,0:T(4,128)S(1)} %copy.9.refs_2_, s32[1,512]{1,0:T(1,128)S(1)} %bitcast.1, s32[1,128]{1,0:T(1,128)S(1)} %copy-done.2), custom_call_target="tpu_custom_call" | custom-call | tf_op jit(solution)/shard_map/pallas_call | solution.py:324
  50.5 0.6 %copy.12 = f32[6,256]{1,0:T(8,128)} copy(f32[6,256]{1,0:T(8,128)S(1)} %get-tuple-element.4) | data formatting | bytes 12288
  51.1 0.6 %copy.13 = f32[3,128]{1,0:T(4,128)} copy(f32[3,128]{1,0:T(4,128)S(1)} %get-tuple-element.5) | data formatting | bytes 3072
  (2 shorter events, 0.0 us)
Async XLA Ops:
  0.6 4.8 %copy-start.2 = (s32[1,128]{1,0:T(1,128)S(1)}, s32[1,128]{1,0:T(1,128)}, u32[]{:S(2)}) copy-start(s32[1,128]{1,0:T(1,128)} %refs_4_.1) | copy-start | bytes 1540
  0.6 4.8 %copy-start.1 = (s32[512]{0:T(512)S(1)}, s32[512]{0:T(512)}, u32[]{:S(2)}) copy-start(s32[512]{0:T(512)} %param.10) | copy-start | bytes 6148
  0.7 4.8 %copy-start.4 = (f32[2,3,512]{2,0,1:T(2,128)S(1)}, f32[2,3,512]{2,0,1:T(2,128)}, u32[]{:S(2)}) copy-start(f32[2,3,512]{2,0,1:T(2,128)} %param.9) | copy-start | bytes 36868
  0.7 4.8 %copy-start.3 = (f32[2,6,512]{2,0,1:T(2,128)S(1)}, f32[2,6,512]{2,0,1:T(2,128)}, u32[]{:S(2)}) copy-start(f32[2,6,512]{2,0,1:T(2,128)} %param.8) | copy-start | bytes 73732
  5.5 0.7 %copy-start = (f32[8,512]{1,0:T(8,128)S(1)}, f32[8,512]{1,0:T(8,128)}, u32[]{:S(2)}) copy-start(f32[8,512]{1,0:T(8,128)} %shard_map.77.refs_0_) | copy-start | bytes 49156
